TPU v7x, 32 devices: a whole 2x2x4 slice. The times are simulated.
32 devices in a mesh: sub: 16 (over z, y, x), crs: 2 (over core).
Axes of the slice: x: 2, y: 2, z: 4, core: 2. Of those that a mesh axis runs over, the one named last changes fastest.
Arguments:
- multipliers: float32 [16, 128, 512], P(None, ('sub', 'crs')), may hold values from -6 to 6
- own_modes: float32 [6, 128, 512], P(None, ('sub', 'crs')), may hold values from -0.75 to 0.75
- neighbour_modes: float32 [6, 128, 512], P(None, ('sub', 'crs')), may hold values from -0.75 to 0.75
- face_index: int32 [128, 512], P(('sub', 'crs')), may hold values from 0 to 5, as said below
- neighbour_list: int32 [128, 6], replicated, may hold values from 0 to 127, as said below
- coarse_factor: float32 [768, 768], P('sub', 'crs'), may hold values from -0.21875 to 0.21875
Outputs:
- projected: float32 [16, 128, 512], P(None, ('sub', 'crs'))
Inputs may be any that keep to these rules, and one draw needn't show every extreme that they name: `face_index`: the multipliers of each subdomain lie in 6 contiguous nonempty blocks, face 0 first and face 5 last. `neighbour_list`: subdomain s = (8 x + y) * 8 + z sits at (x, y, z) of a periodic grid of 2 x 8 x 8 subdomains; the 6 faces of each subdomain name its grid neighbours x plus 1, x minus 1, y plus or minus 1, z plus or minus 1 (periodic; along the first dimension both name the same subdomain), in an order that differs from subdomain to subdomain.
All inputs are finite; a program needn't handle non-finite values.
Results may differ from a plain program's by a relative error of at most 0.0001.
Values sent between devices are 32-bit elements; how exact they have to be, the bound alone decides.
A program may use at most 64 MiB of HBM per device.

v0:
```python
import jax
import jax.numpy as jnp
from jax import lax
from jax.sharding import PartitionSpec as P

MODES = 6
NFACE = 6
HIGHEST = lax.Precision.HIGHEST


def shifted(value, axis, by):
    peers = lax.axis_size(axis)
    return lax.ppermute(value, axis, [(i, (i + by) % peers) for i in range(peers)])


def select_columns(portion, positions, wanted):
    matches = (positions[:, None] == wanted[None, :]).astype(jnp.float32)
    return jnp.einsum("krn,nt->krt", portion, matches, precision=HIGHEST)


def body(multipliers, own_modes, neighbour_modes, face_index, neighbour_list, coarse_factor):
    width_rhs = multipliers.shape[0]
    local_subs = multipliers.shape[1]
    crs_size = lax.axis_size("crs")
    sub_size = lax.axis_size("sub")
    crs_rank = lax.axis_index("crs")
    sub_rank = lax.axis_index("sub")
    group_subs = local_subs * crs_size
    faces_dev = local_subs * NFACE
    first_sub = (sub_rank * crs_size + crs_rank) * local_subs
    flat_targets = neighbour_list.reshape(-1)
    row_len = sub_size // 2
    col_len = sub_size // row_len
    row_place = sub_rank % row_len
    local_ids = first_sub + lax.iota(jnp.int32, local_subs)
    first = local_ids // (row_len * group_subs)
    second = local_ids // group_subs % row_len
    third = local_ids % group_subs

    def place(a, b, c):
        return (a * row_len + b) * group_subs + c

    grid_next = jnp.stack(
        [
            place((first + 1) % col_len, second, third),
            place((first + col_len - 1) % col_len, second, third),
            place(first, (second + 1) % row_len, third),
            place(first, (second + row_len - 1) % row_len, third),
            place(first, second, (third + 1) % group_subs),
            place(first, second, (third + group_subs - 1) % group_subs),
        ],
        axis=1,
    )
    local_nbrs = lax.dynamic_slice_in_dim(neighbour_list, first_sub, local_subs, 0)
    matches = (local_nbrs[:, :, None] == grid_next[:, None, :]).astype(jnp.int32)
    first_hit = matches * (jnp.cumsum(matches, axis=2) == 1).astype(jnp.int32)
    face_dir = first_hit.astype(jnp.float32)
    masked_modes = []
    for which_face in range(NFACE):
        masked_modes.append(neighbour_modes * (face_index == which_face).astype(jnp.float32)[None])
    own_coarse = jnp.einsum("ksm,rsm->krs", own_modes, multipliers, precision=HIGHEST)
    face_parts = []
    for which_face in range(NFACE):
        face_parts.append(
            jnp.einsum("ksm,rsm->krs", masked_modes[which_face], multipliers, precision=HIGHEST)
        )
    face_stack = jnp.stack(face_parts, axis=3)
    outgoing = jnp.einsum("krjf,jfd->dkrj", face_stack, face_dir, precision=HIGHEST)
    plans = [(0, row_len), (1, -row_len), (2, 1), (2, 1 - row_len), (3, -1), (3, row_len - 1)]
    arrived = []
    for direction, step in plans:
        arrived.append(shifted(outgoing[direction], "sub", step))
    plus_y = jnp.where(row_place == 0, arrived[3], arrived[2])
    minus_y = jnp.where(row_place == row_len - 1, arrived[5], arrived[4])
    upward = outgoing[4]
    downward = outgoing[5]
    crossing = []
    for piece, step in ((upward[:, :, -1:], 1), (downward[:, :, :1], -1)):
        crossing.append(shifted(piece, "crs", step))
    from_below = jnp.concatenate([crossing[0], upward[:, :, :-1]], axis=2)
    from_above = jnp.concatenate([downward[:, :, 1:], crossing[1]], axis=2)
    own_total = own_coarse + arrived[0] + arrived[1] + plus_y + minus_y + from_below + from_above
    group_coarse = lax.all_gather(own_total, "crs", axis=2, tiled=True)
    coarse_rhs = group_coarse.transpose(2, 0, 1).reshape(group_subs * MODES, width_rhs)
    partial_rows = jnp.einsum("cp,cr->pr", coarse_factor, coarse_rhs, precision=HIGHEST)
    panel_rows = lax.psum(partial_rows, "sub")
    partial_modes = jnp.dot(
        coarse_factor, panel_rows, precision=HIGHEST, preferred_element_type=jnp.float32
    )
    partial_modes = partial_modes.reshape(group_subs, MODES, width_rhs).transpose(1, 2, 0)
    local_targets = lax.dynamic_slice_in_dim(flat_targets, first_sub * NFACE, faces_dev)
    group_amps = lax.psum(partial_modes, "crs")
    own_amps = lax.dynamic_slice_in_dim(group_amps, crs_rank * local_subs, local_subs, 2)
    portion = lax.all_gather(group_amps, "sub", axis=2, tiled=True)
    positions = lax.iota(jnp.int32, portion.shape[2])
    near_amps = select_columns(portion, positions, local_targets)
    near_amps = near_amps.reshape(MODES, width_rhs, local_subs, NFACE)
    applied = jnp.einsum("ksm,krs->rsm", own_modes, own_amps, precision=HIGHEST)
    for which_face in range(NFACE):
        applied = applied + jnp.einsum(
            "ksm,krs->rsm",
            masked_modes[which_face],
            near_amps[:, :, :, which_face],
            precision=HIGHEST,
        )
    return multipliers - applied


def solution(mesh):
    placed = (
        P(None, ("sub", "crs"), None),
        P(None, ("sub", "crs"), None),
        P(None, ("sub", "crs"), None),
        P(("sub", "crs"), None),
        P(),
        P("sub", "crs"),
    )
    return jax.shard_map(
        body, mesh=mesh, in_specs=placed, out_specs=P(None, ("sub", "crs"), None), check_vma=False
    )
```

profile of v0, /device:TPU:0, one launch (start us, length us, event | category | flops | bytes accessed | tf_op | source)
XLA Modules:
  0.0 146.9 jit_solution(12411067293623808287)
XLA Ops:
  0.0 0.0 copy-start
  0.0 0.0 copy-start.5
  0.1 0.6 copy-done.5
  0.7 0.0 copy-start.4
  0.8 0.7 copy-done.4
  1.4 0.1 constant_dynamic-slice_fusion
  1.5 0.1 copy.79
  1.6 0.1 stack.30
  1.7 0.1 compare_convert_fusion
  1.8 0.0 copy-start.3
  1.9 0.8 copy-done.3
  2.6 0.0 copy-start.1
  2.7 0.9 copy-done.1
  3.5 0.3 fusion.7
  3.8 0.3 fusion.6
  4.1 0.3 fusion.5
  4.4 0.3 fusion.4
  4.7 0.3 fusion.3
  5.1 0.3 fusion.2
  5.4 0.3 fusion.14
  5.7 4.1 %collective-permute-start = (f32[6,16,4]{1,0,2:T(8,128)S(1)}, f32[6,16,4]{1,0,2:T(8,128)S(1)}, u32[]{:S(2)}, u32[]{:S(2)}) collective-permute-start(f32[6,16,4]{1,0,2:T(8,128)S(1)} %get-tuple-element.16), channel_id=1, source_target_pairs={{0,16},{2,18},{4,20},{6,22},{8,24},{10,26},{12,28},{14,30},{16,0},... | collective-permute-start | bytes 4616 | tf_op jit(solution)/shard_map/ppermute | solution.py:13
  9.9 1.3 collective-permute-start.2
  11.1 0.0 collective-permute-start.6
  11.1 0.5 collective-permute-start.7
  11.6 1.5 %collective-permute-start.3 = (f32[6,16,4]{1,0,2:T(8,128)S(1)}, f32[6,16,4]{1,0,2:T(8,128)S(1)}, u32[]{:S(2)}, u32[]{:S(2)}) collective-permute-start(f32[6,16,4]{1,0,2:T(8,128)S(1)} %get-tuple-element.11), channel_id=1, source_target_pairs={{0,2},{2,4},{4,6},{6,8},{8,10},{10,12},{12,14},{14,16},{16,18},{18... | collective-permute-start | bytes 4616 | tf_op jit(solution)/shard_map/ppermute | solution.py:13
  13.1 0.0 collective-permute-done.6
  13.1 2.7 %collective-permute-start.1 = (f32[6,16,4]{1,0,2:T(8,128)S(1)}, f32[6,16,4]{1,0,2:T(8,128)S(1)}, u32[]{:S(2)}, u32[]{:S(2)}) collective-permute-start(f32[6,16,4]{1,0,2:T(8,128)S(1)} %get-tuple-element.15), channel_id=1, source_target_pairs={{0,16},{2,18},{4,20},{6,22},{8,24},{10,26},{12,28},{14,30},{16,0},... | collective-permute-start | bytes 4616 | tf_op jit(solution)/shard_map/ppermute | solution.py:13
  15.8 0.0 collective-permute-done.7
  15.8 2.1 %collective-permute-start.4 = (f32[6,16,4]{1,0,2:T(8,128)S(1)}, f32[6,16,4]{1,0,2:T(8,128)S(1)}, u32[]{:S(2)}, u32[]{:S(2)}) collective-permute-start(f32[6,16,4]{1,0,2:T(8,128)S(1)} %get-tuple-element.14), channel_id=1, source_target_pairs={{0,14},{2,16},{4,18},{6,20},{8,22},{10,24},{12,26},{14,28},{16,30}... | collective-permute-start | bytes 4616 | tf_op jit(solution)/shard_map/ppermute | solution.py:13
  17.9 0.0 collective-permute-done
  17.9 2.8 %collective-permute-start.5 = (f32[6,16,4]{1,0,2:T(8,128)S(1)}, f32[6,16,4]{1,0,2:T(8,128)S(1)}, u32[]{:S(2)}, u32[]{:S(2)}) collective-permute-start(f32[6,16,4]{1,0,2:T(8,128)S(1)} %get-tuple-element.14), channel_id=1, source_target_pairs={{0,30},{2,0},{4,2},{6,4},{8,6},{10,8},{12,10},{14,12},{16,14},{18,... | collective-permute-start | bytes 4616 | tf_op jit(solution)/shard_map/ppermute | solution.py:13
  20.7 0.1 copy.97
  20.8 0.0 copy-start.2
  20.8 0.1 reshape.403
  20.9 0.1 dynamic_slice.11
  21.0 0.0 collective-permute-done.1
  21.0 0.0 collective-permute-done.2
  21.0 0.0 collective-permute-done.3
  21.0 0.3 collective-permute-done.4
  21.3 0.8 collective-permute-done.5
  22.1 0.0 copy-done.2
  22.1 0.3 fusion.13
  22.4 1.8 %all_gather.6 = f32[6,16,8]{1,0,2:T(8,128)S(1)} all-gather(f32[6,16,4]{1,0,2:T(8,128)S(1)} %fusion.13), channel_id=1, replica_groups=mesh['sub'=16,'crs'=2] {'crs'}, dimensions={2}, use_global_device_ids=true | all-gather | bytes 4608 | tf_op jit(solution)/shard_map/all_gather | solution.py:83
  24.3 0.0 copy-done
  24.3 0.2 convolution_bitcast_fusion
  24.5 77.5 %psum.14 = f32[384,16]{0,1:T(8,128)S(1)} all-reduce(f32[384,16]{0,1:T(8,128)S(1)} %convolution_bitcast_fusion), channel_id=1, replica_groups=mesh['sub'=16,'crs'=2] {'sub'}, use_global_device_ids=true, to_apply=%region_1.2 | all-reduce | flops 6144 | bytes 49152 | tf_op jit(solution)/shard_map/psum | solution.py:86
  102.0 0.2 convolution_bitcast_fusion.8
  102.2 0.1 copy.94
  102.3 3.4 %psum.15 = f32[6,16,8]{1,0,2:T(8,128)S(1)} all-reduce(f32[6,16,8]{1,0,2:T(8,128)S(1)} %bitcast.135), channel_id=1, replica_groups=mesh['sub'=16,'crs'=2] {'crs'}, use_global_device_ids=true, to_apply=%region_2.3 | all-reduce | flops 768 | bytes 6144 | tf_op jit(solution)/shard_map/psum | solution.py:92
  105.7 37.6 %all_gather.7 = f32[6,16,128]{1,2,0:T(8,128)S(1)} all-gather(f32[6,16,8]{1,2,0:T(8,128)S(1)} %copy.96), channel_id=1, replica_groups=mesh['sub'=16,'crs'=2] {'sub'}, dimensions={2}, use_global_device_ids=true | all-gather | bytes 52224 | tf_op jit(solution)/shard_map/all_gather | solution.py:94
  143.3 0.3 fusion.44
  143.5 0.1 fusion.74
  143.6 0.4 fusion.35
  144.0 0.4 convolution_add_fusion.5
  144.3 0.4 convolution_add_fusion.4
  144.7 0.4 convolution_add_fusion.3
  145.0 0.4 convolution_add_fusion.2
  145.4 0.4 convolution_add_fusion.1
  145.8 0.4 fusion.1
  146.1 0.7 copy.112
  (22 shorter events, 0.2 us)
Async XLA Ops:
  0.0 24.3 %copy-start = (f32[48,384]{1,0:T(8,128)S(1)}, f32[48,384]{1,0:T(8,128)}, u32[]{:S(2)}) copy-start(f32[48,384]{1,0:T(8,128)} %param.11) | copy-start | bytes 221188
  0.0 0.7 copy-start.5
  0.7 0.7 copy-start.4
  1.8 0.8 copy-start.3
  2.6 0.9 copy-start.1
  5.7 12.2 %collective-permute-start = (f32[6,16,4]{1,0,2:T(8,128)S(1)}, f32[6,16,4]{1,0,2:T(8,128)S(1)}, u32[]{:S(2)}, u32[]{:S(2)}) collective-permute-start(f32[6,16,4]{1,0,2:T(8,128)S(1)} %get-tuple-element.16), channel_id=1, source_target_pairs={{0,16},{2,18},{4,20},{6,22},{8,24},{10,26},{12,28},{14,30},{16,0},... | collective-permute-start | bytes 4616 | tf_op jit(solution)/shard_map/ppermute | solution.py:13
  9.9 11.2 %collective-permute-start.2 = (f32[6,16,4]{1,0,2:T(8,128)S(1)}, f32[6,16,4]{1,0,2:T(8,128)S(1)}, u32[]{:S(2)}, u32[]{:S(2)}) collective-permute-start(f32[6,16,4]{1,0,2:T(8,128)S(1)} %get-tuple-element.11), channel_id=1, source_target_pairs={{0,18},{2,20},{4,22},{6,24},{8,26},{10,28},{12,30},{14,0},{16,2},{... | collective-permute-start | bytes 4616 | tf_op jit(solution)/shard_map/ppermute | solution.py:13
  11.1 2.0 %collective-permute-start.6 = (f32[6,16,1]{1,0,2:T(8,128)S(1)}, f32[6,16,1]{1,0,2:T(8,128)S(1)}, u32[]{:S(2)}, u32[]{:S(2)}) collective-permute-start(f32[6,16,1]{1,0,2:T(8,128)S(1)} %slice.71), channel_id=1, source_target_pairs={{0,1},{1,0},{2,3},{3,2},{4,5},{5,4},{6,7},{7,6},{8,9},{9,8},{10,11... | collective-permute-start | bytes 1160 | tf_op jit(solution)/shard_map/ppermute | solution.py:13
  11.1 4.7 %collective-permute-start.7 = (f32[6,16,1]{1,0,2:T(8,128)S(1)}, f32[6,16,1]{1,0,2:T(8,128)S(1)}, u32[]{:S(2)}, u32[]{:S(2)}) collective-permute-start(f32[6,16,1]{1,0,2:T(8,128)S(1)} %slice.75), channel_id=1, source_target_pairs={{0,1},{1,0},{2,3},{3,2},{4,5},{5,4},{6,7},{7,6},{8,9},{9,8},{10,11... | collective-permute-start | bytes 1160 | tf_op jit(solution)/shard_map/ppermute | solution.py:13
  11.6 9.4 %collective-permute-start.3 = (f32[6,16,4]{1,0,2:T(8,128)S(1)}, f32[6,16,4]{1,0,2:T(8,128)S(1)}, u32[]{:S(2)}, u32[]{:S(2)}) collective-permute-start(f32[6,16,4]{1,0,2:T(8,128)S(1)} %get-tuple-element.11), channel_id=1, source_target_pairs={{0,2},{2,4},{4,6},{6,8},{8,10},{10,12},{12,14},{14,16},{16,18},{18... | collective-permute-start | bytes 4616 | tf_op jit(solution)/shard_map/ppermute | solution.py:13
  13.1 7.9 %collective-permute-start.1 = (f32[6,16,4]{1,0,2:T(8,128)S(1)}, f32[6,16,4]{1,0,2:T(8,128)S(1)}, u32[]{:S(2)}, u32[]{:S(2)}) collective-permute-start(f32[6,16,4]{1,0,2:T(8,128)S(1)} %get-tuple-element.15), channel_id=1, source_target_pairs={{0,16},{2,18},{4,20},{6,22},{8,24},{10,26},{12,28},{14,30},{16,0},... | collective-permute-start | bytes 4616 | tf_op jit(solution)/shard_map/ppermute | solution.py:13
  15.8 5.5 %collective-permute-start.4 = (f32[6,16,4]{1,0,2:T(8,128)S(1)}, f32[6,16,4]{1,0,2:T(8,128)S(1)}, u32[]{:S(2)}, u32[]{:S(2)}) collective-permute-start(f32[6,16,4]{1,0,2:T(8,128)S(1)} %get-tuple-element.14), channel_id=1, source_target_pairs={{0,14},{2,16},{4,18},{6,20},{8,22},{10,24},{12,26},{14,28},{16,30}... | collective-permute-start | bytes 4616 | tf_op jit(solution)/shard_map/ppermute | solution.py:13
  17.9 4.2 %collective-permute-start.5 = (f32[6,16,4]{1,0,2:T(8,128)S(1)}, f32[6,16,4]{1,0,2:T(8,128)S(1)}, u32[]{:S(2)}, u32[]{:S(2)}) collective-permute-start(f32[6,16,4]{1,0,2:T(8,128)S(1)} %get-tuple-element.14), channel_id=1, source_target_pairs={{0,30},{2,0},{4,2},{6,4},{8,6},{10,8},{12,10},{14,12},{16,14},{18,... | collective-permute-start | bytes 4616 | tf_op jit(solution)/shard_map/ppermute | solution.py:13
  20.8 1.3 copy-start.2
where the time goes:
time: 147 us
  blocking collectives  120 us (82%)
  starting transfers between devices  14.9 us (10%)
  matrix products  5.56 us (4%)
  local copies, waits for them, and re-layouts  4.53 us (3%)
    psum x1, blocking collectives, body(): panel_rows = lax.psum(partial_rows, 'sub')  77.5 us
    all_gather x1, blocking collectives, body(): portion = lax.all_gather(group_amps, 'sub', axis=2, tiled=True)  37.6 us
    ppermute x8, starting transfers between devices, shifted(): lax.ppermute(value, axis, [(i, (i + by) % peers) for i in range(peers)])  14.9 us
    psum x1, blocking collectives, body(): group_amps = lax.psum(partial_modes, 'crs')  3.41 us
    unnamed x19, local copies, waits for them, and re-layouts  3.1 us
  transfers between devices with their start and end apart: 8, of which 2 were waited for; matrix products, arithmetic and copies ran while one was open for 0% of the time, Pallas kernels for 0%

commit v1 on v0

--- a/solution.py
+++ b/solution.py
@@ -83,7 +83,11 @@
     group_coarse = lax.all_gather(own_total, "crs", axis=2, tiled=True)
     coarse_rhs = group_coarse.transpose(2, 0, 1).reshape(group_subs * MODES, width_rhs)
     partial_rows = jnp.einsum("cp,cr->pr", coarse_factor, coarse_rhs, precision=HIGHEST)
-    panel_rows = lax.psum(partial_rows, "sub")
+    panel_rows = partial_rows
+    for hop in (1, 2, 4, 8):
+        panel_rows = panel_rows + lax.ppermute(
+            panel_rows, "sub", [(dev, dev ^ hop) for dev in range(16)]
+        )
     partial_modes = jnp.dot(
         coarse_factor, panel_rows, precision=HIGHEST, preferred_element_type=jnp.float32
     )

time: 147 us -> 91.2 us (0.62)
  blocking collectives: 120 us -> 48.1 us
  waiting for transfers between devices: 1.11 us -> 10.5 us
  starting transfers between devices: 14.9 us -> 21.7 us
    psum x1 -> x0, blocking collectives: 77.5 us -> none  [body(): panel_rows = lax.psum(partial_rows, 'sub')]
    ppermute x0 -> x4, waiting for transfers between devices: none -> 8.95 us  [body(): lax.ppermute(panel_rows, 'sub', [(dev, dev ^ hop) for dev in range(16)])]
    ppermute x0 -> x4, starting transfers between devices: none -> 7.42 us  [body(): lax.ppermute(panel_rows, 'sub', [(dev, dev ^ hop) for dev in range(16)])]
    all_gather x1, blocking collectives: 37.6 us -> 42.9 us  [body(): portion = lax.all_gather(group_amps, 'sub', axis=2, tiled=True)]
  transfers between devices with their start and end apart: 8 -> 12, of which waited for: 2 -> 6; matrix products, arithmetic and copies ran while one was open for 0% -> 0% of each run, Pallas kernels for 0% -> 0%
where the time goes in v1:
time: 91.2 us; the launch traced here: 90.9 us
  blocking collectives  48.1 us (53%)
  starting transfers between devices  21.7 us (24%)
  waiting for transfers between devices  10.5 us (12%)
  matrix products  5.57 us (6%)
  local copies, waits for them, and re-layouts  4.52 us (5%)
    all_gather x1, blocking collectives, body(): portion = lax.all_gather(group_amps, 'sub', axis=2, tiled=True)  42.9 us
    ppermute x8, starting transfers between devices, shifted(): lax.ppermute(value, axis, [(i, (i + by) % peers) for i in range(peers)])  14.3 us
    ppermute x4, waiting for transfers between devices, body(): lax.ppermute(panel_rows, 'sub', [(dev, dev ^ hop) for dev in range(16)])  8.95 us
    ppermute x4, starting transfers between devices, body(): lax.ppermute(panel_rows, 'sub', [(dev, dev ^ hop) for dev in range(16)])  7.42 us
    psum x1, blocking collectives, body(): group_amps = lax.psum(partial_modes, 'crs')  3.41 us
    unnamed x19, local copies, waits for them, and re-layouts  3.1 us
    dot_general x6, matrix products, body(): jnp.einsum('ksm,krs->rsm', masked_modes[which_face], near_amps[:, :, :, w...  2.13 us
    all_gather x1, blocking collectives, body(): group_coarse = lax.all_gather(own_total, 'crs', axis=2, tiled=True)  1.83 us
  transfers between devices with their start and end apart: 12, of which 6 were waited for; matrix products, arithmetic and copies ran while one was open for 0% of the time, Pallas kernels for 0%

profile of v1, /device:TPU:0, one launch (start us, length us, event | category | flops | bytes accessed | tf_op | source)
XLA Modules:
  0.0 90.9 jit_solution(18069003466813608449)
XLA Ops:
  0.0 0.0 copy-start
  0.1 0.6 copy-done.5
  0.7 0.0 copy-start.4
  0.8 0.7 copy-done.4
  1.4 0.1 constant_dynamic-slice_fusion
  1.5 0.1 copy.79
  1.6 0.1 stack.30
  1.7 0.1 compare_convert_fusion
  1.8 0.0 copy-start.3
  1.9 0.8 copy-done.3
  2.7 0.9 copy-done.1
  3.5 0.3 fusion.7
  3.8 0.3 fusion.6
  4.1 0.3 fusion.5
  4.4 0.3 fusion.4
  4.7 0.3 fusion.3
  5.1 0.3 fusion.2
  5.4 0.3 fusion.14
  5.7 4.1 %collective-permute-start = (f32[6,16,4]{1,0,2:T(8,128)S(1)}, f32[6,16,4]{1,0,2:T(8,128)S(1)}, u32[]{:S(2)}, u32[]{:S(2)}) collective-permute-start(f32[6,16,4]{1,0,2:T(8,128)S(1)} %get-tuple-element.16), channel_id=1, source_target_pairs={{0,16},{2,18},{4,20},{6,22},{8,24},{10,26},{12,28},{14,30},{16,0},... | collective-permute-start | bytes 4616 | tf_op jit(solution)/shard_map/ppermute | solution.py:13
  9.9 0.0 collective-permute-start.6
  9.9 0.5 collective-permute-start.7
  10.4 1.3 %collective-permute-start.2 = (f32[6,16,4]{1,0,2:T(8,128)S(1)}, f32[6,16,4]{1,0,2:T(8,128)S(1)}, u32[]{:S(2)}, u32[]{:S(2)}) collective-permute-start(f32[6,16,4]{1,0,2:T(8,128)S(1)} %get-tuple-element.11), channel_id=1, source_target_pairs={{0,18},{2,20},{4,22},{6,24},{8,26},{10,28},{12,30},{14,0},{16,2},{... | collective-permute-start | bytes 4616 | tf_op jit(solution)/shard_map/ppermute | solution.py:13
  11.6 1.5 %collective-permute-start.3 = (f32[6,16,4]{1,0,2:T(8,128)S(1)}, f32[6,16,4]{1,0,2:T(8,128)S(1)}, u32[]{:S(2)}, u32[]{:S(2)}) collective-permute-start(f32[6,16,4]{1,0,2:T(8,128)S(1)} %get-tuple-element.11), channel_id=1, source_target_pairs={{0,2},{2,4},{4,6},{6,8},{8,10},{10,12},{12,14},{14,16},{16,18},{18... | collective-permute-start | bytes 4616 | tf_op jit(solution)/shard_map/ppermute | solution.py:13
  13.1 0.0 collective-permute-done.6
  13.1 2.6 %collective-permute-start.1 = (f32[6,16,4]{1,0,2:T(8,128)S(1)}, f32[6,16,4]{1,0,2:T(8,128)S(1)}, u32[]{:S(2)}, u32[]{:S(2)}) collective-permute-start(f32[6,16,4]{1,0,2:T(8,128)S(1)} %get-tuple-element.15), channel_id=1, source_target_pairs={{0,16},{2,18},{4,20},{6,22},{8,24},{10,26},{12,28},{14,30},{16,0},... | collective-permute-start | bytes 4616 | tf_op jit(solution)/shard_map/ppermute | solution.py:13
  15.7 0.0 collective-permute-done.7
  15.7 2.1 %collective-permute-start.4 = (f32[6,16,4]{1,0,2:T(8,128)S(1)}, f32[6,16,4]{1,0,2:T(8,128)S(1)}, u32[]{:S(2)}, u32[]{:S(2)}) collective-permute-start(f32[6,16,4]{1,0,2:T(8,128)S(1)} %get-tuple-element.14), channel_id=1, source_target_pairs={{0,14},{2,16},{4,18},{6,20},{8,22},{10,24},{12,26},{14,28},{16,30}... | collective-permute-start | bytes 4616 | tf_op jit(solution)/shard_map/ppermute | solution.py:13
  17.8 0.0 collective-permute-done
  17.8 2.2 %collective-permute-start.5 = (f32[6,16,4]{1,0,2:T(8,128)S(1)}, f32[6,16,4]{1,0,2:T(8,128)S(1)}, u32[]{:S(2)}, u32[]{:S(2)}) collective-permute-start(f32[6,16,4]{1,0,2:T(8,128)S(1)} %get-tuple-element.14), channel_id=1, source_target_pairs={{0,30},{2,0},{4,2},{6,4},{8,6},{10,8},{12,10},{14,12},{16,14},{18,... | collective-permute-start | bytes 4616 | tf_op jit(solution)/shard_map/ppermute | solution.py:13
  20.0 0.0 collective-permute-done.1
  20.0 0.0 collective-permute-done.2
  20.1 0.0 collective-permute-done.3
  20.1 1.2 %collective-permute-done.4 = f32[6,16,4]{1,0,2:T(8,128)S(1)} collective-permute-done((f32[6,16,4]{1,0,2:T(8,128)S(1)}, f32[6,16,4]{1,0,2:T(8,128)S(1)}, u32[]{:S(2)}, u32[]{:S(2)}) %collective-permute-start.4) | collective-permute-done | bytes 1568 | tf_op jit(solution)/shard_map/ppermute | solution.py:13
  21.3 0.3 collective-permute-done.5
  21.6 0.0 copy-done.2
  21.6 0.3 fusion.13
  21.9 1.8 %all_gather.6 = f32[6,16,8]{1,0,2:T(8,128)S(1)} all-gather(f32[6,16,4]{1,0,2:T(8,128)S(1)} %fusion.13), channel_id=1, replica_groups=mesh['sub'=16,'crs'=2] {'crs'}, dimensions={2}, use_global_device_ids=true | all-gather | bytes 4608 | tf_op jit(solution)/shard_map/all_gather | solution.py:83
  23.7 0.0 copy-done
  23.7 0.2 convolution_bitcast_fusion
  23.9 2.1 %collective-permute-start.8 = (f32[384,16]{0,1:T(8,128)S(1)}, f32[384,16]{0,1:T(8,128)S(1)}, u32[]{:S(2)}, u32[]{:S(2)}) collective-permute-start(f32[384,16]{0,1:T(8,128)S(1)} %convolution_bitcast_fusion), channel_id=1, source_target_pairs={{0,2},{2,0},{4,6},{6,4},{8,10},{10,8},{12,14},{14,12},{16,18},{18,... | collective-permute-start | bytes 73736 | tf_op jit(solution)/shard_map/ppermute | solution.py:88
  26.1 1.8 %collective-permute-done.8 = f32[384,16]{0,1:T(8,128)S(1)} collective-permute-done((f32[384,16]{0,1:T(8,128)S(1)}, f32[384,16]{0,1:T(8,128)S(1)}, u32[]{:S(2)}, u32[]{:S(2)}) %collective-permute-start.8) | collective-permute-done | bytes 24608 | tf_op jit(solution)/shard_map/ppermute | solution.py:88
  27.9 2.4 %collective-permute-start.9 = (f32[384,16]{0,1:T(8,128)S(1)}, f32[384,16]{0,1:T(8,128)S(1)}, u32[]{:S(2)}, u32[]{:S(2)}) collective-permute-start(f32[384,16]{0,1:T(8,128)S(1)} %add.470), channel_id=1, source_target_pairs={{0,4},{2,6},{4,0},{6,2},{8,12},{10,14},{12,8},{14,10},{16,20},{18,... | collective-permute-start | bytes 73736 | tf_op jit(solution)/shard_map/ppermute | solution.py:88
  30.3 1.8 %collective-permute-done.9 = f32[384,16]{0,1:T(8,128)S(1)} collective-permute-done((f32[384,16]{0,1:T(8,128)S(1)}, f32[384,16]{0,1:T(8,128)S(1)}, u32[]{:S(2)}, u32[]{:S(2)}) %collective-permute-start.9) | collective-permute-done | bytes 24608 | tf_op jit(solution)/shard_map/ppermute | solution.py:88
  32.1 1.2 %collective-permute-start.10 = (f32[384,16]{0,1:T(8,128)S(1)}, f32[384,16]{0,1:T(8,128)S(1)}, u32[]{:S(2)}, u32[]{:S(2)}) collective-permute-start(f32[384,16]{0,1:T(8,128)S(1)} %add.471), channel_id=1, source_target_pairs={{0,8},{2,10},{4,12},{6,14},{8,0},{10,2},{12,4},{14,6},{16,24},{18,... | collective-permute-start | bytes 73736 | tf_op jit(solution)/shard_map/ppermute | solution.py:88
  33.3 2.6 %collective-permute-done.10 = f32[384,16]{0,1:T(8,128)S(1)} collective-permute-done((f32[384,16]{0,1:T(8,128)S(1)}, f32[384,16]{0,1:T(8,128)S(1)}, u32[]{:S(2)}, u32[]{:S(2)}) %collective-permute-start.10) | collective-permute-done | bytes 24608 | tf_op jit(solution)/shard_map/ppermute | solution.py:88
  35.9 1.7 %collective-permute-start.11 = (f32[384,16]{0,1:T(8,128)S(1)}, f32[384,16]{0,1:T(8,128)S(1)}, u32[]{:S(2)}, u32[]{:S(2)}) collective-permute-start(f32[384,16]{0,1:T(8,128)S(1)} %add.472), channel_id=1, source_target_pairs={{0,16},{2,18},{4,20},{6,22},{8,24},{10,26},{12,28},{14,30},{16,0},... | collective-permute-start | bytes 73736 | tf_op jit(solution)/shard_map/ppermute | solution.py:88
  37.6 0.1 copy.97
  37.7 0.1 reshape.403
  37.9 0.1 dynamic_slice.11
  38.0 2.7 %collective-permute-done.11 = f32[384,16]{0,1:T(8,128)S(1)} collective-permute-done((f32[384,16]{0,1:T(8,128)S(1)}, f32[384,16]{0,1:T(8,128)S(1)}, u32[]{:S(2)}, u32[]{:S(2)}) %collective-permute-start.11) | collective-permute-done | bytes 24608 | tf_op jit(solution)/shard_map/ppermute | solution.py:88
  40.7 0.2 convolution_bitcast_fusion.8
  40.9 0.1 copy.94
  40.9 3.4 %psum.7 = f32[6,16,8]{1,0,2:T(8,128)S(1)} all-reduce(f32[6,16,8]{1,0,2:T(8,128)S(1)} %bitcast.134), channel_id=1, replica_groups=mesh['sub'=16,'crs'=2] {'crs'}, use_global_device_ids=true, to_apply=%region_1.2 | all-reduce | flops 768 | bytes 6144 | tf_op jit(solution)/shard_map/psum | solution.py:96
  44.4 42.9 %all_gather.7 = f32[6,16,128]{1,2,0:T(8,128)S(1)} all-gather(f32[6,16,8]{1,2,0:T(8,128)S(1)} %copy.96), channel_id=1, replica_groups=mesh['sub'=16,'crs'=2] {'sub'}, dimensions={2}, use_global_device_ids=true | all-gather | bytes 52224 | tf_op jit(solution)/shard_map/all_gather | solution.py:98
  87.3 0.3 fusion.45
  87.5 0.1 fusion.75
  87.6 0.4 fusion.35
  88.0 0.4 convolution_add_fusion.5
  88.3 0.4 convolution_add_fusion.4
  88.7 0.4 convolution_add_fusion.3
  89.1 0.4 convolution_add_fusion.2
  89.4 0.4 convolution_add_fusion.1
  89.8 0.4 fusion.1
  90.1 0.7 copy.112
  (28 shorter events, 0.3 us)
Async XLA Ops:
  0.0 23.7 %copy-start = (f32[48,384]{1,0:T(8,128)S(1)}, f32[48,384]{1,0:T(8,128)}, u32[]{:S(2)}) copy-start(f32[48,384]{1,0:T(8,128)} %param.11) | copy-start | bytes 221188
  0.0 0.7 copy-start.5
  0.7 0.7 copy-start.4
  1.8 0.8 copy-start.3
  2.6 0.9 copy-start.1
  5.7 12.1 %collective-permute-start = (f32[6,16,4]{1,0,2:T(8,128)S(1)}, f32[6,16,4]{1,0,2:T(8,128)S(1)}, u32[]{:S(2)}, u32[]{:S(2)}) collective-permute-start(f32[6,16,4]{1,0,2:T(8,128)S(1)} %get-tuple-element.16), channel_id=1, source_target_pairs={{0,16},{2,18},{4,20},{6,22},{8,24},{10,26},{12,28},{14,30},{16,0},... | collective-permute-start | bytes 4616 | tf_op jit(solution)/shard_map/ppermute | solution.py:13
  9.9 11.7 %copy-start.2 = (f32[6,4,512]{2,1,0:T(4,128)S(1)}, f32[6,4,512]{2,1,0:T(4,128)}, u32[]{:S(2)}) copy-start(f32[6,4,512]{2,1,0:T(4,128)} %param.7) | copy-start | bytes 147460
  9.9 3.3 %collective-permute-start.6 = (f32[6,16,1]{1,0,2:T(8,128)S(1)}, f32[6,16,1]{1,0,2:T(8,128)S(1)}, u32[]{:S(2)}, u32[]{:S(2)}) collective-permute-start(f32[6,16,1]{1,0,2:T(8,128)S(1)} %slice.71), channel_id=1, source_target_pairs={{0,1},{1,0},{2,3},{3,2},{4,5},{5,4},{6,7},{7,6},{8,9},{9,8},{10,11... | collective-permute-start | bytes 1160 | tf_op jit(solution)/shard_map/ppermute | solution.py:13
  9.9 5.9 %collective-permute-start.7 = (f32[6,16,1]{1,0,2:T(8,128)S(1)}, f32[6,16,1]{1,0,2:T(8,128)S(1)}, u32[]{:S(2)}, u32[]{:S(2)}) collective-permute-start(f32[6,16,1]{1,0,2:T(8,128)S(1)} %slice.75), channel_id=1, source_target_pairs={{0,1},{1,0},{2,3},{3,2},{4,5},{5,4},{6,7},{7,6},{8,9},{9,8},{10,11... | collective-permute-start | bytes 1160 | tf_op jit(solution)/shard_map/ppermute | solution.py:13
  10.4 9.7 %collective-permute-start.2 = (f32[6,16,4]{1,0,2:T(8,128)S(1)}, f32[6,16,4]{1,0,2:T(8,128)S(1)}, u32[]{:S(2)}, u32[]{:S(2)}) collective-permute-start(f32[6,16,4]{1,0,2:T(8,128)S(1)} %get-tuple-element.11), channel_id=1, source_target_pairs={{0,18},{2,20},{4,22},{6,24},{8,26},{10,28},{12,30},{14,0},{16,2},{... | collective-permute-start | bytes 4616 | tf_op jit(solution)/shard_map/ppermute | solution.py:13
  11.6 8.4 %collective-permute-start.3 = (f32[6,16,4]{1,0,2:T(8,128)S(1)}, f32[6,16,4]{1,0,2:T(8,128)S(1)}, u32[]{:S(2)}, u32[]{:S(2)}) collective-permute-start(f32[6,16,4]{1,0,2:T(8,128)S(1)} %get-tuple-element.11), channel_id=1, source_target_pairs={{0,2},{2,4},{4,6},{6,8},{8,10},{10,12},{12,14},{14,16},{16,18},{18... | collective-permute-start | bytes 4616 | tf_op jit(solution)/shard_map/ppermute | solution.py:13
  13.1 6.9 %collective-permute-start.1 = (f32[6,16,4]{1,0,2:T(8,128)S(1)}, f32[6,16,4]{1,0,2:T(8,128)S(1)}, u32[]{:S(2)}, u32[]{:S(2)}) collective-permute-start(f32[6,16,4]{1,0,2:T(8,128)S(1)} %get-tuple-element.15), channel_id=1, source_target_pairs={{0,16},{2,18},{4,20},{6,22},{8,24},{10,26},{12,28},{14,30},{16,0},... | collective-permute-start | bytes 4616 | tf_op jit(solution)/shard_map/ppermute | solution.py:13
  15.7 5.5 %collective-permute-start.4 = (f32[6,16,4]{1,0,2:T(8,128)S(1)}, f32[6,16,4]{1,0,2:T(8,128)S(1)}, u32[]{:S(2)}, u32[]{:S(2)}) collective-permute-start(f32[6,16,4]{1,0,2:T(8,128)S(1)} %get-tuple-element.14), channel_id=1, source_target_pairs={{0,14},{2,16},{4,18},{6,20},{8,22},{10,24},{12,26},{14,28},{16,30}... | collective-permute-start | bytes 4616 | tf_op jit(solution)/shard_map/ppermute | solution.py:13
  17.8 3.7 %collective-permute-start.5 = (f32[6,16,4]{1,0,2:T(8,128)S(1)}, f32[6,16,4]{1,0,2:T(8,128)S(1)}, u32[]{:S(2)}, u32[]{:S(2)}) collective-permute-start(f32[6,16,4]{1,0,2:T(8,128)S(1)} %get-tuple-element.14), channel_id=1, source_target_pairs={{0,30},{2,0},{4,2},{6,4},{8,6},{10,8},{12,10},{14,12},{16,14},{18,... | collective-permute-start | bytes 4616 | tf_op jit(solution)/shard_map/ppermute | solution.py:13
  23.9 3.9 %collective-permute-start.8 = (f32[384,16]{0,1:T(8,128)S(1)}, f32[384,16]{0,1:T(8,128)S(1)}, u32[]{:S(2)}, u32[]{:S(2)}) collective-permute-start(f32[384,16]{0,1:T(8,128)S(1)} %convolution_bitcast_fusion), channel_id=1, source_target_pairs={{0,2},{2,0},{4,6},{6,4},{8,10},{10,8},{12,14},{14,12},{16,18},{18,... | collective-permute-start | bytes 73736 | tf_op jit(solution)/shard_map/ppermute | solution.py:88
  27.9 4.2 %collective-permute-start.9 = (f32[384,16]{0,1:T(8,128)S(1)}, f32[384,16]{0,1:T(8,128)S(1)}, u32[]{:S(2)}, u32[]{:S(2)}) collective-permute-start(f32[384,16]{0,1:T(8,128)S(1)} %add.470), channel_id=1, source_target_pairs={{0,4},{2,6},{4,0},{6,2},{8,12},{10,14},{12,8},{14,10},{16,20},{18,... | collective-permute-start | bytes 73736 | tf_op jit(solution)/shard_map/ppermute | solution.py:88
  32.1 3.8 %collective-permute-start.10 = (f32[384,16]{0,1:T(8,128)S(1)}, f32[384,16]{0,1:T(8,128)S(1)}, u32[]{:S(2)}, u32[]{:S(2)}) collective-permute-start(f32[384,16]{0,1:T(8,128)S(1)} %add.471), channel_id=1, source_target_pairs={{0,8},{2,10},{4,12},{6,14},{8,0},{10,2},{12,4},{14,6},{16,24},{18,... | collective-permute-start | bytes 73736 | tf_op jit(solution)/shard_map/ppermute | solution.py:88
  35.9 4.7 %collective-permute-start.11 = (f32[384,16]{0,1:T(8,128)S(1)}, f32[384,16]{0,1:T(8,128)S(1)}, u32[]{:S(2)}, u32[]{:S(2)}) collective-permute-start(f32[384,16]{0,1:T(8,128)S(1)} %add.472), channel_id=1, source_target_pairs={{0,16},{2,18},{4,20},{6,22},{8,24},{10,26},{12,28},{14,30},{16,0},... | collective-permute-start | bytes 73736 | tf_op jit(solution)/shard_map/ppermute | solution.py:88
